TPU v7x, 512 devices: a whole 4x4x16 slice. The times are simulated.
512 devices in a mesh: strip: 32 (over z, core), front: 16 (over y, x).
Axes of the slice: x: 4, y: 4, z: 16, core: 2. Of those that a mesh axis runs over, the one named last changes fastest.
Arguments:
- topmost_facet_vertex_table: int32 [32, 1024, 3], P('strip', 'front'), may hold values from 0 to 2047, as said below
- neighbour_bottom_vertex_table: int32 [32, 1024, 3], P('strip', 'front'), may hold values from 0 to 2047, as said below
- topmost_facet_forcing: bfloat16 [32, 1024, 6, 128], P('strip', 'front'), may hold values from -6 to 6
- bottom_facet_forcing: bfloat16 [32, 1024, 6, 128], P('strip', 'front'), may hold values from -6 to 6
- interior_unknown_forcing: bfloat16 [32, 1024, 128], P('strip', 'front'), may hold values from -6 to 6
- interior_elimination_matrix: bfloat16 [32, 1024, 4096], P('strip', 'front'), may hold values from -0.1875 to 0.1875
- border_interaction_matrix: bfloat16 [32, 4096, 4096], P('strip', None, 'front'), may hold values from -0.0625 to 0.0625
- reciprocal_diagonal_factor: bfloat16 [32, 4096, 4096], P('strip', 'front'), may hold values from -0.2 to 1.5
- initial_received_border: bfloat16 [32, 32, 4096], P('strip', None, 'front'), may hold values from -6 to 6
Outputs:
- fronts: bfloat16 [32, 4, 32, 4096], P('strip', None, None, 'front')
Inputs may be any that keep to these rules, and one draw needn't show every extreme that they name: `topmost_facet_vertex_table`: row e of a strip lists the node numbers of the three edge nodes of element e (corner, midside, corner), in that front's own node order, with 2048 nodes on a front. `neighbour_bottom_vertex_table`: row e of strip s lists the three edge nodes of element e of strip s + 1's bottom row, in strip s's front node order.
All inputs are finite; a program needn't handle non-finite values.
Results may differ from a plain program's by a relative error of at most 0.0075.
Values may be sent and summed in bfloat16 or wider, within the bound.
A program may use at most 64 MiB of HBM per device.

v0:
```python
import jax
import jax.numpy as jnp
from jax import lax
from jax.sharding import PartitionSpec as P

STEPS = 4


def shifted(block, axis, distance):
    devices = range(lax.axis_size(axis))
    route = [(i - distance, i) for i in devices if i - distance in devices]
    return lax.ppermute(block, axis, route)


def copy_for_each(array, axis):
    count = lax.axis_size(axis)
    return lax.all_to_all(
        jnp.broadcast_to(array[None], (count, *array.shape)), axis, 0, 0, tiled=True
    )


def joined_along(tiles, dim):
    shape = list(tiles.shape[1:])
    shape[dim] *= tiles.shape[0]
    return jnp.moveaxis(tiles, 0, dim).reshape(shape)


def gather_directly(array, axis, dim):
    tiles = copy_for_each(array, axis)
    return joined_along(tiles, dim)


def cut_along(array, dim, count):
    before, after = (array.shape[:dim], array.shape[dim + 1 :])
    return jnp.moveaxis(array.reshape(*before, count, -1, *after), dim, 0)


def summed_on_arrival(array, axis, dim):
    count = lax.axis_size(axis)
    tiles = lax.all_to_all(cut_along(array, dim, count), axis, 0, 0, tiled=True)
    return jnp.sum(tiles, axis=0)


def incidence(node_ids, dof_rows):
    dof_ids = (2 * node_ids[:, :, None] + jnp.arange(2, dtype=jnp.int32)[None, None, :]).reshape(-1)
    return (dof_rows[:, None] == dof_ids[None, :]).astype(jnp.bfloat16)


def shards(
    topmost_facet_vertex_table,
    neighbour_bottom_vertex_table,
    topmost_facet_forcing,
    bottom_facet_forcing,
    interior_unknown_forcing,
    interior_elimination_matrix,
    border_interaction_matrix,
    reciprocal_diagonal_factor,
    initial_received_border,
):
    panel_cols = border_interaction_matrix.shape[2]
    grouped_scenario_forcing = initial_received_border.shape[1]
    all_cases = topmost_facet_forcing.shape[3]
    upper_loads = shifted(bottom_facet_forcing[0], "strip", -1)
    own_flat = topmost_facet_forcing[0].reshape(-1, all_cases)
    upper_flat = upper_loads.reshape(-1, all_cases)
    dof_rows = jnp.arange(panel_cols * lax.axis_size("front"), dtype=jnp.int32)
    assembled = jnp.dot(
        incidence(topmost_facet_vertex_table[0], dof_rows),
        own_flat,
        preferred_element_type=jnp.float32,
    )
    assembled = assembled + jnp.dot(
        incidence(neighbour_bottom_vertex_table[0], dof_rows),
        upper_flat,
        preferred_element_type=jnp.float32,
    )
    condense_cols = interior_elimination_matrix[0]
    interior_part = lax.dot_general(
        condense_cols,
        interior_unknown_forcing[0],
        (((0,), (0,)), ((), ())),
        preferred_element_type=jnp.float32,
    )
    load_panel = lax.psum_scatter(
        assembled - interior_part, "front", scatter_dimension=0, tiled=True
    )
    load_panel = load_panel.T
    couple_panel = border_interaction_matrix[0]
    inverse_panel = reciprocal_diagonal_factor[0]
    results = []
    front_share = initial_received_border[0]
    for window_step in range(STEPS):
        incoming_border_forcing = gather_directly(front_share, "front", 1)
        case_loads = load_panel[
            window_step * grouped_scenario_forcing : (window_step + 1) * grouped_scenario_forcing
        ]
        reduced = (
            case_loads
            - jnp.dot(incoming_border_forcing, couple_panel, preferred_element_type=jnp.float32)
        ).astype(jnp.bfloat16)
        partials = jnp.dot(reduced, inverse_panel, preferred_element_type=jnp.float32)
        outgoing = summed_on_arrival(partials, "front", 1).astype(jnp.bfloat16)
        results.append(outgoing)
        if window_step + 1 < STEPS:
            front_share = shifted(outgoing, "strip", 1)
    return jnp.stack(results, 0)[None]


def solution(mesh):
    return jax.shard_map(
        shards,
        mesh=mesh,
        in_specs=(
            P("strip", "front", None),
            P("strip", "front", None),
            P("strip", "front", None, None),
            P("strip", "front", None, None),
            P("strip", "front", None),
            P("strip", "front", None),
            P("strip", None, "front"),
            P("strip", "front", None),
            P("strip", None, "front"),
        ),
        out_specs=P("strip", None, None, "front"),
        check_vma=False,
    )
```

profile of v0, /device:TPU:96, one launch (start us, length us, event | category | flops | bytes accessed | tf_op | source)
XLA Modules:
  0.0 244.8 jit_solution(13186957021052479573)
XLA Ops:
  6.5 0.0 copy-start
  6.5 0.0 reduce-scatter.2.cloned.1.call-start
  6.5 2.0 collective-permute-start
  8.6 1.0 copy.53
  9.6 0.7 broadcast_multiply_fusion.1
  10.3 0.1 copy.70
  10.4 0.1 iota_add_fusion.1
  10.5 0.1 add.48
  10.7 0.7 broadcast_multiply_fusion
  11.4 0.1 copy.71
  11.5 0.0 copy-start.1
  11.5 0.0 copy-start.3
  11.5 2.8 %fusion = f32[4096,128]{0,1:T(8,128)} fusion(bf16[384,128]{1,0:T(8,128)(2,1)S(1)} %reshape_squeeze.3, s32[384]{0:T(512)S(1)} %add.48), kind=kOutput, calls=%fused_computation.2 | convolution fusion | flops 404226048 | bytes 2196992 | tf_op jit(solution)/shard_map/dot_general | solution.py:67
  14.2 0.0 copy-done.1
  14.2 0.0 copy-done.3
  14.2 1.8 fusion.58
  16.0 0.1 iota_add_fusion
  16.2 0.1 add.52
  16.3 0.0 collective-permute-done
  16.3 0.1 copy.55
  16.4 5.0 %fusion.3 = f32[4096,128]{0,1:T(8,128)} fusion(f32[4096,128]{0,1:T(8,128)} %fusion.58, f32[4096,128]{0,1:T(8,128)} %fusion, bf16[384,128]{1,0:T(8,128)(2,1)S(1)} %reshape.104, s32[384]{0:T(512)S(1)} %add.52), kind=kOutput, calls=%fused_computation.5 | convolution fusion | flops 405274624 | bytes 6391296 | tf_op jit(solution)/shard_map/dot_general | solution.py:72
  21.5 0.0 copy-start.4
  21.5 0.0 reduce-scatter.2.cloned.1.call-update
  21.5 0.7 copy-done.4
  22.2 0.7 broadcast_in_dim.13
  22.9 7.0 %all-to-all-start = ((bf16[16,32,256]{2,1,0:T(8,128)(2,1)}), bf16[16,32,256]{2,1,0:T(8,128)(2,1)S(1)}, u32[]{:S(2)}, u32[]{:S(2)}) async-start(bf16[16,32,256]{2,1,0:T(8,128)(2,1)} %broadcast_in_dim.13), calls=%async_computation.1 | async-start | bytes 524288 | tf_op jit(solution)/shard_map/all_to_all | solution.py:17
  30.0 4.1 %copy.72 = bf16[4096,256]{1,0:T(8,128)(2,1)} copy(bf16[4096,256]{0,1:T(8,128)(2,1)} %bitcast.114) | data formatting | bytes 4194304 | tf_op jit(solution)/shard_map/dot_general | solution.py:101
  34.1 5.2 %all-to-all-done = bf16[16,32,256]{2,1,0:T(8,128)(2,1)S(1)} async-done(((bf16[16,32,256]{2,1,0:T(8,128)(2,1)}), bf16[16,32,256]{2,1,0:T(8,128)(2,1)S(1)}, u32[]{:S(2)}, u32[]{:S(2)}) %all-to-all-start) | async-done | bytes 262176 | tf_op jit(solution)/shard_map/all_to_all | solution.py:17
  39.3 76.5 %reduce-scatter.2.cloned.1.call-done = f32[256,128]{0,1:T(8,128)} async-done(((f32[4096,128]{0,1:T(8,128)}), f32[256,128]{0,1:T(8,128)}) %reduce-scatter.2.cloned.1.call-update) | async-done | bytes 131088 | tf_op jit(solution)/shard_map/reduce_scatter | solution.py:84
  115.8 0.0 copy-done
  115.8 3.1 %convolution_bitcast_fusion.3 = f32[16,32,256]{2,1,0:T(8,128)S(1)} fusion(bf16[16,256,256]{2,1,0:T(8,128)(2,1)} %bitcast.110, bf16[32,4096]{1,0:T(8,128)(2,1)S(1)} %bitcast.115, bf16[1,4096,256]{2,1,0:T(8,128)(2,1)S(1)} %copy-done, f32[128,256]{1,0:T(8,128)} %bitcast.123), kind=kOutput, calls=%fused_computation.19 | convolution fusion | flops 134234112 | bytes 5013504 | tf_op jit(solution)/shard_map/dot_general | solution.py:101
  118.9 0.0 copy-start.2
  118.9 15.0 %all_to_all.40 = f32[16,32,256]{2,1,0:T(8,128)S(1)} all-to-all(f32[16,32,256]{2,1,0:T(8,128)S(1)} %convolution_bitcast_fusion.3), channel_id=1, replica_groups=mesh['strip'=32,'front'=16] {'front'}, dimensions={0} | all-to-all | bytes 1048576 | tf_op jit(solution)/shard_map/all_to_all | solution.py:40
  134.0 1.9 collective-permute-start.1
  135.9 3.1 %collective-permute-done.1 = bf16[32,256]{1,0:T(8,128)(2,1)S(1)} collective-permute-done((bf16[32,256]{1,0:T(8,128)(2,1)S(1)}, bf16[32,256]{1,0:T(8,128)(2,1)S(1)}, u32[]{:S(2)}, u32[]{:S(2)}) %collective-permute-start.1) | collective-permute-done | bytes 16416 | tf_op jit(solution)/shard_map/ppermute | solution.py:12
  139.1 12.4 %all_to_all.41 = bf16[16,32,256]{2,1,0:T(8,128)(2,1)S(1)} all-to-all(bf16[16,32,256]{2,1,0:T(8,128)(2,1)S(1)} %broadcast_in_dim.14), channel_id=1, replica_groups=mesh['strip'=32,'front'=16] {'front'}, dimensions={0} | all-to-all | bytes 524288 | tf_op jit(solution)/shard_map/all_to_all | solution.py:17
  151.5 0.0 copy-done.2
  151.6 3.1 %convolution_bitcast_fusion.2 = f32[16,32,256]{2,1,0:T(8,128)S(1)} fusion(bf16[16,256,256]{2,1,0:T(8,128)(2,1)} %bitcast.111, bf16[32,4096]{1,0:T(8,128)(2,1)S(1)} %bitcast.117, bf16[1,4096,256]{2,1,0:T(8,128)(2,1)S(1)} %copy-done, f32[128,256]{1,0:T(8,128)S(1)} %bitcast.124), kind=kOutput, calls=%fused_computation.18 | convolution fusion | flops 134234112 | bytes 5013504 | tf_op jit(solution)/shard_map/dot_general | solution.py:101
  154.7 14.1 %all_to_all.42 = f32[16,32,256]{2,1,0:T(8,128)S(1)} all-to-all(f32[16,32,256]{2,1,0:T(8,128)S(1)} %convolution_bitcast_fusion.2), channel_id=1, replica_groups=mesh['strip'=32,'front'=16] {'front'}, dimensions={0} | all-to-all | bytes 1048576 | tf_op jit(solution)/shard_map/all_to_all | solution.py:40
  168.9 1.9 collective-permute-start.2
  170.8 3.1 %collective-permute-done.2 = bf16[32,256]{1,0:T(8,128)(2,1)S(1)} collective-permute-done((bf16[32,256]{1,0:T(8,128)(2,1)S(1)}, bf16[32,256]{1,0:T(8,128)(2,1)S(1)}, u32[]{:S(2)}, u32[]{:S(2)}) %collective-permute-start.2) | collective-permute-done | bytes 16416 | tf_op jit(solution)/shard_map/ppermute | solution.py:12
  174.0 11.8 %all_to_all.43 = bf16[16,32,256]{2,1,0:T(8,128)(2,1)S(1)} all-to-all(bf16[16,32,256]{2,1,0:T(8,128)(2,1)S(1)} %broadcast_in_dim.15), channel_id=1, replica_groups=mesh['strip'=32,'front'=16] {'front'}, dimensions={0} | all-to-all | bytes 524288 | tf_op jit(solution)/shard_map/all_to_all | solution.py:17
  185.7 3.1 %convolution_bitcast_fusion.1 = f32[16,32,256]{2,1,0:T(8,128)S(1)} fusion(bf16[16,256,256]{2,1,0:T(8,128)(2,1)} %bitcast.112, bf16[32,4096]{1,0:T(8,128)(2,1)S(1)} %bitcast.118, bf16[1,4096,256]{2,1,0:T(8,128)(2,1)S(1)} %copy-done, f32[128,256]{1,0:T(8,128)S(1)} %bitcast.125), kind=kOutput, calls=%fused_computation.17 | convolution fusion | flops 134234112 | bytes 5013504 | tf_op jit(solution)/shard_map/dot_general | solution.py:101
  188.9 13.5 %all_to_all.44 = f32[16,32,256]{2,1,0:T(8,128)S(1)} all-to-all(f32[16,32,256]{2,1,0:T(8,128)S(1)} %convolution_bitcast_fusion.1), channel_id=1, replica_groups=mesh['strip'=32,'front'=16] {'front'}, dimensions={0} | all-to-all | bytes 1048576 | tf_op jit(solution)/shard_map/all_to_all | solution.py:40
  202.4 1.9 collective-permute-start.3
  204.3 3.1 %collective-permute-done.3 = bf16[32,256]{1,0:T(8,128)(2,1)S(1)} collective-permute-done((bf16[32,256]{1,0:T(8,128)(2,1)S(1)}, bf16[32,256]{1,0:T(8,128)(2,1)S(1)}, u32[]{:S(2)}, u32[]{:S(2)}) %collective-permute-start.3) | collective-permute-done | bytes 16416 | tf_op jit(solution)/shard_map/ppermute | solution.py:12
  207.4 12.4 %all_to_all.45 = bf16[16,32,256]{2,1,0:T(8,128)(2,1)S(1)} all-to-all(bf16[16,32,256]{2,1,0:T(8,128)(2,1)S(1)} %broadcast_in_dim.16), channel_id=1, replica_groups=mesh['strip'=32,'front'=16] {'front'}, dimensions={0} | all-to-all | bytes 524288 | tf_op jit(solution)/shard_map/all_to_all | solution.py:17
  219.9 3.1 %convolution_bitcast_fusion = f32[16,32,256]{2,1,0:T(8,128)S(1)} fusion(bf16[16,256,256]{2,1,0:T(8,128)(2,1)} %bitcast.113, bf16[32,4096]{1,0:T(8,128)(2,1)S(1)} %bitcast.116, bf16[1,4096,256]{2,1,0:T(8,128)(2,1)S(1)} %copy-done, f32[128,256]{1,0:T(8,128)S(1)} %bitcast.126), kind=kOutput, calls=%fused_computation.16 | convolution fusion | flops 134234112 | bytes 5013504 | tf_op jit(solution)/shard_map/dot_general | solution.py:101
  223.0 14.2 %all_to_all.46 = f32[16,32,256]{2,1,0:T(8,128)S(1)} all-to-all(f32[16,32,256]{2,1,0:T(8,128)S(1)} %convolution_bitcast_fusion), channel_id=1, replica_groups=mesh['strip'=32,'front'=16] {'front'}, dimensions={0} | all-to-all | bytes 1048576 | tf_op jit(solution)/shard_map/all_to_all | solution.py:40
  237.3 0.6 maximum_bitcast_fusion
  (13 shorter events, 0.4 us)
Async XLA Ops:
  6.5 109.3 %copy-start = (bf16[1,4096,256]{2,1,0:T(8,128)(2,1)S(1)}, bf16[1,4096,256]{2,1,0:T(8,128)(2,1)}, u32[]{:S(2)}) copy-start(bf16[1,4096,256]{2,1,0:T(8,128)(2,1)} %param.15) | copy-start | bytes 6291460
  6.5 109.3 %reduce-scatter.2.cloned.1.call-start = ((), (), s32[]{:S(2)}) async-start(), calls=%async_computation.9 | async-start | bytes 2228224 | tf_op jit(solution)/shard_map/reduce_scatter | solution.py:84
  6.5 9.8 %collective-permute-start = (bf16[64,6,128]{2,0,1:T(8,128)(2,1)}, bf16[64,6,128]{2,0,1:T(8,128)(2,1)S(1)}, u32[]{:S(2)}, u32[]{:S(2)}) collective-permute-start(bf16[64,6,128]{2,0,1:T(8,128)(2,1)} %bitcast.134), channel_id=1, source_target_pairs={{16,0},{32,16},{48,32},{64,48},{80,64},{96,80},{112,96},{128,112},... | collective-permute-start | bytes 294920 | tf_op jit(solution)/shard_map/ppermute | solution.py:12
  11.5 2.8 %copy-start.1 = (bf16[1,64,4096]{2,1,0:T(8,128)(2,1)S(1)}, bf16[1,64,4096]{2,1,0:T(8,128)(2,1)}, u32[]{:S(2)}) copy-start(bf16[1,64,4096]{2,1,0:T(8,128)(2,1)} %param.14) | copy-start | bytes 1572868
  11.5 2.8 %copy-start.3 = (bf16[1,64,128]{2,1,0:T(8,128)(2,1)S(1)}, bf16[1,64,128]{2,1,0:T(8,128)(2,1)}, u32[]{:S(2)}) copy-start(bf16[1,64,128]{2,1,0:T(8,128)(2,1)} %param.13) | copy-start | bytes 49156
  21.5 0.7 copy-start.4
  22.9 16.4 %all-to-all-start = ((bf16[16,32,256]{2,1,0:T(8,128)(2,1)}), bf16[16,32,256]{2,1,0:T(8,128)(2,1)S(1)}, u32[]{:S(2)}, u32[]{:S(2)}) async-start(bf16[16,32,256]{2,1,0:T(8,128)(2,1)} %broadcast_in_dim.13), calls=%async_computation.1 | async-start | bytes 524288 | tf_op jit(solution)/shard_map/all_to_all | solution.py:17
  118.9 32.6 %copy-start.2 = (f32[256,128]{0,1:T(8,128)S(1)}, f32[256,128]{0,1:T(8,128)}, u32[]{:S(2)}) copy-start(f32[256,128]{0,1:T(8,128)} %reduce-scatter.2.cloned.1.call-done) | copy-start | bytes 393220
  134.0 5.1 %collective-permute-start.1 = (bf16[32,256]{1,0:T(8,128)(2,1)S(1)}, bf16[32,256]{1,0:T(8,128)(2,1)S(1)}, u32[]{:S(2)}, u32[]{:S(2)}) collective-permute-start(bf16[32,256]{1,0:T(8,128)(2,1)S(1)} %reduce_sum.36), channel_id=1, source_target_pairs={{0,16},{16,32},{32,48},{48,64},{64,80},{80,96},{96,112},{112,128},... | collective-permute-start | bytes 49160 | tf_op jit(solution)/shard_map/ppermute | solution.py:12
  168.9 5.1 %collective-permute-start.2 = (bf16[32,256]{1,0:T(8,128)(2,1)S(1)}, bf16[32,256]{1,0:T(8,128)(2,1)S(1)}, u32[]{:S(2)}, u32[]{:S(2)}) collective-permute-start(bf16[32,256]{1,0:T(8,128)(2,1)S(1)} %reduce_sum.37), channel_id=1, source_target_pairs={{0,16},{16,32},{32,48},{48,64},{64,80},{80,96},{96,112},{112,128},... | collective-permute-start | bytes 49160 | tf_op jit(solution)/shard_map/ppermute | solution.py:12
  202.4 5.1 %collective-permute-start.3 = (bf16[32,256]{1,0:T(8,128)(2,1)S(1)}, bf16[32,256]{1,0:T(8,128)(2,1)S(1)}, u32[]{:S(2)}, u32[]{:S(2)}) collective-permute-start(bf16[32,256]{1,0:T(8,128)(2,1)S(1)} %reduce_sum.38), channel_id=1, source_target_pairs={{0,16},{16,32},{32,48},{48,64},{64,80},{80,96},{96,112},{112,128},... | collective-permute-start | bytes 49160 | tf_op jit(solution)/shard_map/ppermute | solution.py:12
Sparse Core Ops, SparseCore 0:
  21.6 94.1 reduce-scatter.1
where the time goes:
time: 246 us; the launch traced here: 245 us
  blocking collectives  93.5 us (38%)
  waiting for transfers between devices  91.1 us (37%)
  matrix products  22.1 us (9%)
  starting transfers between devices  14.8 us (6%)
  between operations  13.5 us (5%)
  local copies, waits for them, and re-layouts  7.27 us (3%)
    reduce_scatter x1, waiting for transfers between devices, shards(): lax.psum_scatter(assembled - interior_part, 'front', scatter_dimension=0,...  76.5 us
    all_to_all x4, blocking collectives, summed_on_arrival(): tiles = lax.all_to_all(cut_along(array, dim, count), axis, 0, 0, tiled=True)  56.9 us
    all_to_all x3, blocking collectives, copy_for_each(): lax.all_to_all(jnp.broadcast_to(array[None], (count, *array.shape)), axis...  36.6 us
    dot_general x4, matrix products, shards(): jnp.dot(reduced, inverse_panel, preferred_element_type=jnp.float32)  12.5 us
    ppermute x4, waiting for transfers between devices, shifted(): return lax.ppermute(block, axis, route)  9.39 us
    ppermute x4, starting transfers between devices, shifted(): return lax.ppermute(block, axis, route)  7.8 us
    all_to_all x1, starting transfers between devices, copy_for_each(): lax.all_to_all(jnp.broadcast_to(array[None], (count, *array.shape)), axis...  7.03 us
    all_to_all x1, waiting for transfers between devices, copy_for_each(): lax.all_to_all(jnp.broadcast_to(array[None], (count, *array.shape)), axis...  5.23 us
  transfers between devices with their start and end apart: 6, of which 5 were waited for; matrix products, arithmetic and copies ran while one was open for 5% of the time, Pallas kernels for 0%

commit v1 on v0

v1 whole, which is shorter than its diff:
```python
import functools

import jax
import jax.numpy as jnp
from jax import lax
from jax.experimental import pallas as pl
from jax.experimental.pallas import tpu as pltpu
from jax.sharding import PartitionSpec as P

MESH = pl.DeviceIdType.MESH
STEPS = 4
SIDE = 4
F32, BF16 = jnp.float32, jnp.bfloat16


def ring_gap(step):
    return min(step, SIDE - step)


def reach(k):
    return ring_gap(k // SIDE) + ring_gap(k % SIDE)


def kernel(
    strips,
    fronts,
    own_table,
    low_table,
    top_loads,
    bottom_loads,
    inner_loads,
    condense,
    couple_hbm,
    inverse_hbm,
    first_front,
    out,
    couple,
    inverse,
    own_nodes,
    low_nodes,
    upper,
    lhs_own,
    lhs_up,
    partial,
    load_send,
    load_own,
    load_slots,
    front_slots,
    sum_send,
    sum_slots,
    weight_sem,
    upper_sems,
    load_sems,
    load_send_sems,
    front_sems,
    front_send_sems,
    sum_sems,
    sum_send_sems,
):
    strip, front = lax.axis_index("strip"), lax.axis_index("front")
    row, col = front // SIDE, front % SIDE
    group, width = first_front.shape
    cases = inner_loads.shape[1]
    far_first = sorted(range(1, fronts), key=lambda k: -reach(k))
    near_first = sorted(range(1, fronts), key=reach)

    def ahead(k):
        return ((row + k // SIDE) % SIDE) * SIDE + (col + k % SIDE) % SIDE

    def behind(k):
        return ((row + SIDE - k // SIDE) % SIDE) * SIDE + (col + SIDE - k % SIDE) % SIDE

    def send(src, dst, send_sem, recv_sem, where):
        return pltpu.make_async_remote_copy(
            src_ref=src,
            dst_ref=dst,
            send_sem=send_sem,
            recv_sem=recv_sem,
            device_id=where,
            device_id_type=MESH,
        )

    def landed(ref, sem):
        pltpu.make_async_copy(ref, ref, sem).wait()

    load_weights = [
        pltpu.make_async_copy(couple_hbm, couple, weight_sem.at[0]),
        pltpu.make_async_copy(inverse_hbm, inverse, weight_sem.at[1]),
    ]
    for copy in load_weights:
        copy.start()

    barrier = pltpu.get_barrier_semaphore()
    for k in near_first:
        pl.semaphore_signal(barrier, 1, device_id=(strip, ahead(k)), device_id_type=MESH)

    @pl.when(strip < strips - 1)
    def _():
        pl.semaphore_signal(barrier, 1, device_id=(strip + 1, front), device_id_type=MESH)

    @pl.when(strip > 0)
    def _():
        pl.semaphore_signal(barrier, 1, device_id=(strip - 1, front), device_id_type=MESH)

    def incidence(table, columns):
        start = columns * width
        dofs = lax.broadcasted_iota(jnp.int32, (table.shape[0], width), 1) + start
        tiles = []
        for j in range(6):
            ids = 2 * table[:, j // 2 : j // 2 + 1] + j % 2
            tiles.append(jnp.where(dofs == ids, 1.0, 0.0).astype(BF16))
        return jnp.concatenate(tiles, axis=0)

    def turned(loads):
        return loads[...].reshape(-1, cases).astype(F32).T

    edge_rows = 6 * top_loads.shape[1]
    own_nodes[...] = own_table[:, 0].T
    low_nodes[...] = low_table[:, 0].T
    lhs_own[:, :edge_rows] = turned(top_loads).astype(BF16)
    lhs_own[:, edge_rows:] = (-inner_loads[...].astype(F32).T).astype(BF16)

    @pl.loop(0, fronts)
    def _(k):
        where = ahead(k)
        at = pl.ds(pl.multiple_of(where * width, width), width)
        rhs = jnp.concatenate([incidence(own_nodes, where), condense[:, at]], axis=0)
        partial[k] = jnp.dot(lhs_own[...], rhs, preferred_element_type=F32)

    below = jnp.minimum(strip, 1)
    above = jnp.minimum(strips - 1 - strip, 1)
    pl.semaphore_wait(barrier, fronts - 1 + below + above)

    @pl.when(strip > 0)
    def _():
        send(bottom_loads, upper, upper_sems.at[0], upper_sems.at[1], (strip - 1, front)).start()

    for k in far_first:
        send(
            first_front,
            front_slots.at[0, k],
            front_send_sems.at[0],
            front_sems.at[0, k],
            (strip, ahead(k)),
        ).start()
    front_slots[0, 0] = first_front[...]

    @pl.when(strip == 0)
    def _():
        for step in range(1, STEPS):
            front_slots[step] = jnp.zeros_like(front_slots[step])

    @pl.when(strip == strips - 1)
    def _():
        upper[...] = jnp.zeros_like(upper)

    @pl.when(strip < strips - 1)
    def _():
        landed(upper, upper_sems.at[1])

    lhs_up[...] = turned(upper).astype(BF16)

    def load_copy(step, k, where):
        return send(
            load_send.at[k, step],
            load_slots.at[step, k],
            load_send_sems.at[step],
            load_sems.at[step, k],
            (strip, where),
        )

    @pl.loop(0, fronts - 1)
    def _(i):
        k = (i + 10) % (fronts - 1) + 1
        where = ahead(k)
        both = partial[k] + jnp.dot(
            lhs_up[...], incidence(low_nodes, where), preferred_element_type=F32
        )
        load_send[k] = both.astype(BF16).reshape(STEPS, group, width)
        load_copy(0, k, where).start()

    both = partial[0] + jnp.dot(lhs_up[...], incidence(low_nodes, front), preferred_element_type=F32)
    load_own[...] = both.reshape(STEPS, group, width)

    for copy in load_weights:
        copy.wait()

    @pl.loop(0, STEPS)
    def _(step):
        joined = jnp.zeros((group, width), F32)
        for k in [0, *near_first]:
            if k == 0:
                expected = (step > 0) & (strip > 0)
            else:
                expected = (step == 0) | (strip > 0)

            @pl.when(expected)
            def _():
                landed(front_slots.at[step, k], front_sems.at[step, k])

            at = pl.ds(pl.multiple_of(behind(k) * width, width), width)
            joined = joined + jnp.dot(
                front_slots[step, k], couple[at, :], preferred_element_type=F32
            )

        total = load_own[step]
        for k in near_first:
            landed(load_slots.at[step, k], load_sems.at[step, k])
            total = total + load_slots[step, k].astype(F32)
        reduced = (total - joined).astype(BF16)

        for k in far_first:
            where = ahead(k)
            at = pl.ds(pl.multiple_of(where * width, width), width)
            sum_send[step, k] = jnp.dot(
                reduced, inverse[:, at], preferred_element_type=F32
            ).astype(BF16)
            send(
                sum_send.at[step, k],
                sum_slots.at[step, k],
                sum_send_sems.at[step],
                sum_sems.at[step, k],
                (strip, where),
            ).start()

        @pl.when(step < STEPS - 1)
        def _():
            for k in far_first:
                load_copy(step + 1, k, ahead(k)).start()

        at = pl.ds(pl.multiple_of(front * width, width), width)
        summed = jnp.dot(reduced, inverse[:, at], preferred_element_type=F32)
        for k in near_first:
            landed(sum_slots.at[step, k], sum_sems.at[step, k])
            summed = summed + sum_slots[step, k].astype(F32)
        out[step] = summed.astype(BF16)

        @pl.when((step < STEPS - 1) & (strip < strips - 1))
        def _():
            for k in [*far_first, 0]:
                send(
                    out.at[step],
                    front_slots.at[step + 1, k],
                    front_send_sems.at[step + 1],
                    front_sems.at[step + 1, k],
                    (strip + 1, ahead(k)),
                ).start()

    @pl.when(strip > 0)
    def _():
        landed(upper, upper_sems.at[0])

    landed(front_slots.at[0, pl.ds(1, fronts - 1)], front_send_sems.at[0])
    for step in range(STEPS):
        landed(sum_slots.at[step, pl.ds(1, fronts - 1)], sum_send_sems.at[step])
        landed(load_slots.at[step, pl.ds(1, fronts - 1)], load_send_sems.at[step])

    @pl.when(strip < strips - 1)
    def _():
        for step in range(1, STEPS):
            landed(front_slots.at[step], front_send_sems.at[step])


def solution(mesh):
    strips, fronts = mesh.shape["strip"], mesh.shape["front"]

    def shards(*blocks):
        tables = [jnp.transpose(block, (2, 0, 1)) for block in blocks[:2]]
        blocks = tables + [block[0] for block in blocks[2:]]
        for i in (2, 3):
            blocks[i] = jnp.swapaxes(blocks[i], 0, 1)
        elements = blocks[2].shape[1]
        inner, cases = blocks[4].shape
        dofs, width = blocks[6].shape
        group = blocks[8].shape[0]
        in_vmem = pl.BlockSpec(memory_space=pltpu.VMEM)
        in_hbm = pl.BlockSpec(memory_space=pl.ANY)
        slots = pltpu.VMEM((STEPS, fronts, group, width), BF16)
        dma = pltpu.SemaphoreType.DMA
        result = pl.pallas_call(
            functools.partial(kernel, strips, fronts),
            out_shape=jax.ShapeDtypeStruct((STEPS, group, width), BF16),
            in_specs=[in_vmem] * 6 + [in_hbm] * 2 + [in_vmem],
            out_specs=in_vmem,
            scratch_shapes=[
                pltpu.VMEM((dofs, width), BF16),
                pltpu.VMEM((width, dofs), BF16),
                pltpu.VMEM((elements, 3), jnp.int32),
                pltpu.VMEM((elements, 3), jnp.int32),
                pltpu.VMEM((6, elements, cases), BF16),
                pltpu.VMEM((cases, 6 * elements + inner), BF16),
                pltpu.VMEM((cases, 6 * elements), BF16),
                pltpu.VMEM((fronts, cases, width), F32),
                pltpu.VMEM((fronts, STEPS, group, width), BF16),
                pltpu.VMEM((STEPS, group, width), F32),
                slots,
                slots,
                slots,
                slots,
                dma((2,)),
                dma((2,)),
                dma((STEPS, fronts)),
                dma((STEPS,)),
                dma((STEPS, fronts)),
                dma((STEPS,)),
                dma((STEPS, fronts)),
                dma((STEPS,)),
            ],
            compiler_params=pltpu.CompilerParams(collective_id=0, has_side_effects=True),
        )(*blocks)
        return result[None]

    return jax.shard_map(
        shards,
        mesh=mesh,
        in_specs=(
            P("strip", "front", None),
            P("strip", "front", None),
            P("strip", "front", None, None),
            P("strip", "front", None, None),
            P("strip", "front", None),
            P("strip", "front", None),
            P("strip", None, "front"),
            P("strip", "front", None),
            P("strip", None, "front"),
        ),
        out_specs=P("strip", None, None, "front"),
        check_vma=False,
    )
```

time: 246 us -> 74.7 us (0.30)
  the two profiles are of different devices: /device:TPU:96 before, /device:TPU:288 now
where the time goes in v1:
time: 74.7 us; the launch traced here: 74.5 us
  Pallas kernels  73 us (98%)
  local copies, waits for them, and re-layouts  1.47 us (2%)
    pallas_call x1, Pallas kernels, shards(): pl.pallas_call(functools.partial(kernel, strips, fronts), out_shape=jax.S...  73 us

profile of v1, /device:TPU:288, one launch (start us, length us, event | category | flops | bytes accessed | tf_op | source)
XLA Modules:
  0.0 74.5 jit_solution(3072128972663628508)
XLA Ops:
  0.0 73.0 %shard_map.91 = bf16[4,32,256]{2,1,0:T(8,128)(2,1)} custom-call(s32[3,1,64]{2,1,0:T(1,128)} %bitcast.22, s32[3,1,64]{2,1,0:T(1,128)} %bitcast.23, bf16[6,64,128]{2,1,0:T(8,128)(2,1)} %bitcast.18, bf16[6,64,128]{2,1,0:T(8,128)(2,1)} %bitcast.19, bf16[64,128]{1,0:T(8,128)(2,1)} %bitcast.20, bf16[64,4096]{1,0:T(8,128)(2,1)} %bitcast.16, ...), custom_call_target="tpu_custom_call" | custom-call | tf_op jit(solution)/shard_map/pallas_call | solution.py:280
  73.0 1.5 %copy.11 = bf16[1,4,32,256]{3,2,1,0:T(8,128)(2,1)} copy(bf16[1,4,32,256]{3,2,1,0:T(8,128)(2,1)} %bitcast.17) | data formatting | bytes 131072

commit v2 on v1

v2 whole, which is shorter than its diff:
```python
import functools

import jax
import jax.numpy as jnp
from jax import lax
from jax.experimental import pallas as pl
from jax.experimental.pallas import tpu as pltpu
from jax.sharding import PartitionSpec as P

MESH = pl.DeviceIdType.MESH
STEPS = 4
SIDE = 4
F32, BF16 = jnp.float32, jnp.bfloat16


def ring_gap(step):
    return min(step, SIDE - step)


def reach(k):
    return ring_gap(k // SIDE) + ring_gap(k % SIDE)


def kernel(
    strips,
    fronts,
    own_table_hbm,
    low_table_hbm,
    top_hbm,
    bottom_hbm,
    inner_hbm,
    condense_hbm,
    couple_hbm,
    inverse_hbm,
    first_hbm,
    out,
    own_table,
    low_table,
    top_loads,
    bottom_loads,
    inner_loads,
    condense,
    couple,
    inverse,
    first_front,
    own_nodes,
    low_nodes,
    upper,
    lhs_own,
    lhs_up,
    low_marks,
    partial,
    load_send,
    load_own,
    load_slots,
    front_slots,
    sum_send,
    sum_slots,
    input_sems,
    upper_sems,
    load_sems,
    tile_sems,
    near_sems,
    far_sems,
    sum_sems,
    send_sems,
):
    strip, front = lax.axis_index("strip"), lax.axis_index("front")
    row, col = front // SIDE, front % SIDE
    group, width = first_front.shape
    cases = inner_loads.shape[1]
    peers = sorted(range(1, fronts), key=lambda k: -reach(k))
    far = [k for k in peers if reach(k) > 2]
    near = [k for k in peers if reach(k) <= 2]
    batches = [far, near[: len(near) // 2], near[len(near) // 2 :]]
    across = strip % 2

    def ahead(k):
        return ((row + k // SIDE) % SIDE) * SIDE + (col + k % SIDE) % SIDE

    def behind(k):
        return ((row + SIDE - k // SIDE) % SIDE) * SIDE + (col + SIDE - k % SIDE) % SIDE

    def panel(where):
        return pl.ds(pl.multiple_of(where * width, width), width)

    def send(src, dst, send_sem, recv_sem, where):
        pltpu.make_async_remote_copy(
            src_ref=src,
            dst_ref=dst,
            send_sem=send_sem,
            recv_sem=recv_sem,
            device_id=where,
            device_id_type=MESH,
        ).start()

    def landed(ref, sem):
        pltpu.make_async_copy(ref, ref, sem).wait()

    barrier = pltpu.get_barrier_semaphore()
    for k in peers:
        pl.semaphore_signal(barrier, 1, device_id=(strip, ahead(k)), device_id_type=MESH)

    @pl.when(strip < strips - 1)
    def _():
        pl.semaphore_signal(barrier, 1, device_id=(strip + 1, front), device_id_type=MESH)

    @pl.when(strip > 0)
    def _():
        pl.semaphore_signal(barrier, 1, device_id=(strip - 1, front), device_id_type=MESH)

    fetches = [
        pltpu.make_async_copy(src, dst, input_sems.at[i])
        for i, (src, dst) in enumerate(
            [
                (own_table_hbm, own_table),
                (top_hbm, top_loads),
                (inner_hbm, inner_loads),
                (condense_hbm, condense),
                (bottom_hbm, bottom_loads),
                (first_hbm, first_front),
                (low_table_hbm, low_table),
                (couple_hbm, couple),
                (inverse_hbm, inverse),
            ]
        )
    ]
    for copy in fetches:
        copy.start()

    def incidence(table, columns):
        dofs = lax.broadcasted_iota(jnp.int32, (table.shape[0], width), 1) + columns * width
        tiles = []
        for j in range(6):
            ids = 2 * table[:, j // 2 : j // 2 + 1] + j % 2
            tiles.append(jnp.where(dofs == ids, 1.0, 0.0).astype(BF16))
        return jnp.concatenate(tiles, axis=0)

    def turned(loads):
        return loads[...].reshape(-1, cases).astype(F32).T

    edge_rows = 6 * top_loads.shape[1]
    for copy in fetches[:4]:
        copy.wait()
    own_nodes[...] = own_table[:, 0].T
    lhs_own[:, :edge_rows] = turned(top_loads).astype(BF16)
    lhs_own[:, edge_rows:] = (-inner_loads[...].astype(F32).T).astype(BF16)

    @pl.loop(0, fronts)
    def _(k):
        where = ahead(k)
        rhs = jnp.concatenate([incidence(own_nodes, where), condense[:, panel(where)]], axis=0)
        partial[k] = jnp.dot(lhs_own[...], rhs, preferred_element_type=F32)

    for copy in fetches[4:7]:
        copy.wait()

    below = jnp.minimum(strip, 1)
    above = jnp.minimum(strips - 1 - strip, 1)
    pl.semaphore_wait(barrier, fronts - 1 + below + above)

    @pl.when(strip > 0)
    def _():
        send(bottom_loads, upper, upper_sems.at[0], upper_sems.at[1], (strip - 1, front))

    def gather_sem(step, k):
        return (near_sems if k in near else far_sems).at[step]

    for k in peers:
        send(
            first_front,
            front_slots.at[0, k],
            send_sems.at[0],
            gather_sem(0, k),
            (strip, ahead(k)),
        )
    front_slots[0, 0] = first_front[...]

    @pl.when(strip == 0)
    def _():
        for step in range(1, STEPS):
            front_slots[step] = jnp.zeros_like(front_slots[step])

    @pl.when(strip == strips - 1)
    def _():
        upper[...] = jnp.zeros_like(upper)

    low_nodes[...] = low_table[:, 0].T

    @pl.loop(0, fronts)
    def _(k):
        low_marks[k] = incidence(low_nodes, ahead(k))

    @pl.when(strip < strips - 1)
    def _():
        landed(upper, upper_sems.at[1])

    lhs_up[...] = turned(upper).astype(BF16)

    def loads_of(k, rows):
        return partial[k, rows] + jnp.dot(lhs_up[rows], low_marks[k], preferred_element_type=F32)

    def send_loads(step, ks):
        for k in ks:
            send(
                load_send.at[step, k],
                load_slots.at[step, k],
                send_sems.at[1],
                load_sems.at[step],
                (strip, ahead(k)),
            )

    for batch in batches:
        for k in batch:
            load_send[0, k] = loads_of(k, slice(0, group)).astype(BF16)
        send_loads(0, batch)
    load_own[0] = loads_of(0, slice(0, group))

    @pl.loop(0, fronts)
    def _(k):
        rest = loads_of(k, slice(group, cases)).astype(BF16)
        for step in range(1, STEPS):
            load_send[step, k] = rest[(step - 1) * group : step * group]

    rest = loads_of(0, slice(group, cases))
    for step in range(1, STEPS):
        load_own[step] = rest[(step - 1) * group : step * group]

    for copy in fetches[7:]:
        copy.wait()

    @pl.loop(0, STEPS)
    def _(step):
        @pl.when((step > 0) & (strip > 0))
        def _():
            landed(front_slots.at[step, 0], tile_sems.at[step])

        @pl.when((step > 0) & (strip > 0) & (across == 0))
        def _():
            for k in peers:
                send(
                    front_slots.at[step, 0],
                    front_slots.at[step, k],
                    send_sems.at[2],
                    gather_sem(step, k),
                    (strip, ahead(k)),
                )

        def joined_with(ks):
            return functools.reduce(
                jnp.add,
                [
                    jnp.dot(
                        front_slots[step, k],
                        couple[panel(behind(k)), :],
                        preferred_element_type=F32,
                    )
                    for k in ks
                ],
            )

        expected = (step == 0) | (strip > 0)

        @pl.when(expected)
        def _():
            landed(front_slots.at[step, pl.ds(0, len(near))], near_sems.at[step])

        joined = joined_with([0, *near])

        @pl.when(expected)
        def _():
            landed(front_slots.at[step, pl.ds(0, len(far))], far_sems.at[step])

        joined = joined + joined_with(far)

        landed(load_slots.at[step, pl.ds(1, fronts - 1)], load_sems.at[step])
        total = load_own[step]
        for k in peers:
            total = total + load_slots[step, k].astype(F32)
        reduced = (total - joined).astype(BF16)

        def sums_for(where):
            return jnp.dot(reduced, inverse[:, panel(where)], preferred_element_type=F32)

        for batch in batches:
            for k in batch:
                sum_send[step, k] = sums_for(ahead(k)).astype(BF16)
            for k in batch:
                send(
                    sum_send.at[step, k],
                    sum_slots.at[step, k],
                    send_sems.at[3],
                    sum_sems.at[step],
                    (strip, ahead(k)),
                )
        summed = sums_for(front)

        @pl.when(step < STEPS - 1)
        def _():
            send_loads(step + 1, peers)

        landed(sum_slots.at[step, pl.ds(1, fronts - 1)], sum_sems.at[step])
        for k in peers:
            summed = summed + sum_slots[step, k].astype(F32)
        out[step] = summed.astype(BF16)

        onward = (step < STEPS - 1) & (strip < strips - 1)

        @pl.when(onward & (across == 0))
        def _():
            for k in [*far, *near, 0]:
                send(
                    out.at[step],
                    front_slots.at[step + 1, k],
                    send_sems.at[4],
                    tile_sems.at[step + 1] if k == 0 else gather_sem(step + 1, k),
                    (strip + 1, ahead(k)),
                )

        @pl.when(onward & (across == 1))
        def _():
            send(
                out.at[step],
                front_slots.at[step + 1, 0],
                send_sems.at[4],
                tile_sems.at[step + 1],
                (strip + 1, front),
            )

    @pl.when(strip > 0)
    def _():
        landed(upper, upper_sems.at[0])

    others = pl.ds(1, fronts - 1)
    landed(front_slots.at[0, others], send_sems.at[0])
    landed(load_slots.at[:, others], send_sems.at[1])
    landed(sum_slots.at[:, others], send_sems.at[3])

    @pl.when((strip > 0) & (across == 0))
    def _():
        landed(front_slots.at[pl.ds(1, STEPS - 1), others], send_sems.at[2])

    @pl.when((strip < strips - 1) & (across == 0))
    def _():
        landed(front_slots.at[pl.ds(1, STEPS - 1)], send_sems.at[4])

    @pl.when((strip < strips - 1) & (across == 1))
    def _():
        landed(front_slots.at[pl.ds(1, STEPS - 1), 0], send_sems.at[4])


def solution(mesh):
    strips, fronts = mesh.shape["strip"], mesh.shape["front"]

    def shards(*blocks):
        tables = [jnp.transpose(block, (2, 0, 1)) for block in blocks[:2]]
        blocks = tables + [block[0] for block in blocks[2:]]
        for i in (2, 3):
            blocks[i] = jnp.swapaxes(blocks[i], 0, 1)
        elements = blocks[2].shape[1]
        inner, cases = blocks[4].shape
        group, width = blocks[8].shape
        in_vmem = pl.BlockSpec(memory_space=pltpu.VMEM)
        in_hbm = pl.BlockSpec(memory_space=pl.ANY)
        slots = pltpu.VMEM((STEPS, fronts, group, width), BF16)
        dma = pltpu.SemaphoreType.DMA
        result = pl.pallas_call(
            functools.partial(kernel, strips, fronts),
            out_shape=jax.ShapeDtypeStruct((STEPS, group, width), BF16),
            in_specs=[in_hbm] * len(blocks),
            out_specs=in_vmem,
            scratch_shapes=[
                *[pltpu.VMEM(block.shape, block.dtype) for block in blocks],
                pltpu.VMEM((elements, 3), jnp.int32),
                pltpu.VMEM((elements, 3), jnp.int32),
                pltpu.VMEM((6, elements, cases), BF16),
                pltpu.VMEM((cases, 6 * elements + inner), BF16),
                pltpu.VMEM((cases, 6 * elements), BF16),
                pltpu.VMEM((fronts, 6 * elements, width), BF16),
                pltpu.VMEM((fronts, cases, width), F32),
                slots,
                pltpu.VMEM((STEPS, group, width), F32),
                slots,
                slots,
                slots,
                slots,
                dma((len(blocks),)),
                dma((2,)),
                dma((STEPS,)),
                dma((STEPS,)),
                dma((STEPS,)),
                dma((STEPS,)),
                dma((STEPS,)),
                dma((5,)),
            ],
            compiler_params=pltpu.CompilerParams(collective_id=0, has_side_effects=True),
        )(*blocks)
        return result[None]

    return jax.shard_map(
        shards,
        mesh=mesh,
        in_specs=(
            P("strip", "front", None),
            P("strip", "front", None),
            P("strip", "front", None, None),
            P("strip", "front", None, None),
            P("strip", "front", None),
            P("strip", "front", None),
            P("strip", None, "front"),
            P("strip", "front", None),
            P("strip", None, "front"),
        ),
        out_specs=P("strip", None, None, "front"),
        check_vma=False,
    )
```

time: 74.7 us -> 69.9 us (0.936)
  the two profiles are of different devices: /device:TPU:288 before, /device:TPU:384 now
where the time goes in v2:
time: 69.9 us; the launch traced here: 69.8 us
  Pallas kernels  68.3 us (98%)
  local copies, waits for them, and re-layouts  1.47 us (2%)
    pallas_call x1, Pallas kernels, shards(): pl.pallas_call(functools.partial(kernel, strips, fronts), out_shape=jax.S...  68.3 us
    unnamed x1, local copies, waits for them, and re-layouts  1.47 us

profile of v2, /device:TPU:384, one launch (start us, length us, event | category | flops | bytes accessed | tf_op | source)
XLA Modules:
  0.0 69.8 jit_solution(1622209330521316868)
XLA Ops:
  0.0 68.3 %shard_map.91 = bf16[4,32,256]{2,1,0:T(8,128)(2,1)} custom-call(s32[3,1,64]{2,1,0:T(1,128)} %bitcast.22, s32[3,1,64]{2,1,0:T(1,128)} %bitcast.23, bf16[6,64,128]{2,1,0:T(8,128)(2,1)} %bitcast.18, bf16[6,64,128]{2,1,0:T(8,128)(2,1)} %bitcast.19, bf16[64,128]{1,0:T(8,128)(2,1)} %bitcast.20, bf16[64,4096]{1,0:T(8,128)(2,1)} %bitcast.16, ...), custom_call_target="tpu_custom_call" | custom-call | tf_op jit(solution)/shard_map/pallas_call | solution.py:367
  68.3 1.5 %copy.11 = bf16[1,4,32,256]{3,2,1,0:T(8,128)(2,1)} copy(bf16[1,4,32,256]{3,2,1,0:T(8,128)(2,1)} %bitcast.17) | data formatting | bytes 131072

commit v3 on v2

--- a/solution.py
+++ b/solution.py
@@ -43,8 +43,8 @@
     couple,
     inverse,
     first_front,
-    own_nodes,
-    low_nodes,
+    own_ids,
+    low_ids,
     upper,
     lhs_own,
     lhs_up,
@@ -56,6 +56,7 @@
     front_slots,
     sum_send,
     sum_slots,
+    sum_own,
     input_sems,
     upper_sems,
     load_sems,
@@ -113,13 +114,13 @@
         pltpu.make_async_copy(src, dst, input_sems.at[i])
         for i, (src, dst) in enumerate(
             [
+                (low_table_hbm, low_table),
                 (own_table_hbm, own_table),
+                (bottom_hbm, bottom_loads),
+                (first_hbm, first_front),
                 (top_hbm, top_loads),
                 (inner_hbm, inner_loads),
                 (condense_hbm, condense),
-                (bottom_hbm, bottom_loads),
-                (first_hbm, first_front),
-                (low_table_hbm, low_table),
                 (couple_hbm, couple),
                 (inverse_hbm, inverse),
             ]
@@ -128,31 +129,36 @@
     for copy in fetches:
         copy.start()
 
-    def incidence(table, columns):
-        dofs = lax.broadcasted_iota(jnp.int32, (table.shape[0], width), 1) + columns * width
-        tiles = []
+    def spread(table, ids):
+        nodes = table[:, 0].T
         for j in range(6):
-            ids = 2 * table[:, j // 2 : j // 2 + 1] + j % 2
-            tiles.append(jnp.where(dofs == ids, 1.0, 0.0).astype(BF16))
-        return jnp.concatenate(tiles, axis=0)
+            column = 2 * nodes[:, j // 2 : j // 2 + 1] + j % 2
+            ids[j] = jnp.broadcast_to(column, ids.shape[1:])
+
+    def incidence(ids, columns):
+        lanes = ids.shape[2]
+        dofs = lax.broadcasted_iota(jnp.int32, ids.shape[1:], 1) + columns * width
+        halves = [
+            jnp.concatenate(
+                [jnp.where(dofs + start == ids[j], 1.0, 0.0).astype(BF16) for j in range(6)], axis=0
+            )
+            for start in range(0, width, lanes)
+        ]
+        return jnp.concatenate(halves, axis=1)
 
     def turned(loads):
         return loads[...].reshape(-1, cases).astype(F32).T
 
-    edge_rows = 6 * top_loads.shape[1]
-    for copy in fetches[:4]:
+    for copy in fetches[:2]:
         copy.wait()
-    own_nodes[...] = own_table[:, 0].T
-    lhs_own[:, :edge_rows] = turned(top_loads).astype(BF16)
-    lhs_own[:, edge_rows:] = (-inner_loads[...].astype(F32).T).astype(BF16)
-
-    @pl.loop(0, fronts)
+    spread(low_table, low_ids)
+    spread(own_table, own_ids)
+
+    @pl.loop(0, fronts, unroll=4)
     def _(k):
-        where = ahead(k)
-        rhs = jnp.concatenate([incidence(own_nodes, where), condense[:, panel(where)]], axis=0)
-        partial[k] = jnp.dot(lhs_own[...], rhs, preferred_element_type=F32)
-
-    for copy in fetches[4:7]:
+        low_marks[k] = incidence(low_ids, ahead(k))
+
+    for copy in fetches[2:7]:
         copy.wait()
 
     below = jnp.minimum(strip, 1)
@@ -163,17 +169,21 @@
     def _():
         send(bottom_loads, upper, upper_sems.at[0], upper_sems.at[1], (strip - 1, front))
 
-    def gather_sem(step, k):
-        return (near_sems if k in near else far_sems).at[step]
-
-    for k in peers:
-        send(
-            first_front,
-            front_slots.at[0, k],
-            send_sems.at[0],
-            gather_sem(0, k),
-            (strip, ahead(k)),
-        )
+    half = group // 2
+    halves = [pl.ds(h * half, half) for h in (0, 1)]
+
+    def gather_sem(step, k, h):
+        return (near_sems if k in near else far_sems).at[step, h]
+
+    for h, rows in enumerate(halves):
+        for k in peers:
+            send(
+                first_front.at[rows],
+                front_slots.at[0, k, rows],
+                send_sems.at[0],
+                gather_sem(0, k, h),
+                (strip, ahead(k)),
+            )
     front_slots[0, 0] = first_front[...]
 
     @pl.when(strip == 0)
@@ -185,11 +195,15 @@
     def _():
         upper[...] = jnp.zeros_like(upper)
 
-    low_nodes[...] = low_table[:, 0].T
-
-    @pl.loop(0, fronts)
+    edge_rows = 6 * top_loads.shape[1]
+    lhs_own[:, :edge_rows] = turned(top_loads).astype(BF16)
+    lhs_own[:, edge_rows:] = (-inner_loads[...].astype(F32).T).astype(BF16)
+
+    @pl.loop(0, fronts, unroll=2)
     def _(k):
-        low_marks[k] = incidence(low_nodes, ahead(k))
+        where = ahead(k)
+        rhs = jnp.concatenate([incidence(own_ids, where), condense[:, panel(where)]], axis=0)
+        partial[k] = jnp.dot(lhs_own[...], rhs, preferred_element_type=F32)
 
     @pl.when(strip < strips - 1)
     def _():
@@ -200,23 +214,24 @@
     def loads_of(k, rows):
         return partial[k, rows] + jnp.dot(lhs_up[rows], low_marks[k], preferred_element_type=F32)
 
-    def send_loads(step, ks):
+    def send_loads(step, rows, sem, ks):
         for k in ks:
             send(
-                load_send.at[step, k],
-                load_slots.at[step, k],
+                load_send.at[step, k, rows],
+                load_slots.at[step, k, rows],
                 send_sems.at[1],
-                load_sems.at[step],
+                sem,
                 (strip, ahead(k)),
             )
 
     for batch in batches:
         for k in batch:
             load_send[0, k] = loads_of(k, slice(0, group)).astype(BF16)
-        send_loads(0, batch)
+        send_loads(0, halves[0], load_sems.at[0], batch)
+    send_loads(0, halves[1], load_sems.at[STEPS], peers)
     load_own[0] = loads_of(0, slice(0, group))
 
-    @pl.loop(0, fronts)
+    @pl.loop(0, fronts, unroll=2)
     def _(k):
         rest = loads_of(k, slice(group, cases)).astype(BF16)
         for step in range(1, STEPS):
@@ -229,29 +244,31 @@
     for copy in fetches[7:]:
         copy.wait()
 
+    others = pl.ds(1, fronts - 1)
+
     @pl.loop(0, STEPS)
     def _(step):
-        @pl.when((step > 0) & (strip > 0))
-        def _():
-            landed(front_slots.at[step, 0], tile_sems.at[step])
-
         @pl.when((step > 0) & (strip > 0) & (across == 0))
         def _():
-            for k in peers:
-                send(
-                    front_slots.at[step, 0],
-                    front_slots.at[step, k],
-                    send_sems.at[2],
-                    gather_sem(step, k),
-                    (strip, ahead(k)),
-                )
-
-        def joined_with(ks):
+            for h, rows in enumerate(halves):
+                landed(front_slots.at[step, 0, rows], tile_sems.at[step, h])
+                for k in peers:
+                    send(
+                        front_slots.at[step, 0, rows],
+                        front_slots.at[step, k, rows],
+                        send_sems.at[2],
+                        gather_sem(step, k, h),
+                        (strip, ahead(k)),
+                    )
+
+        expected = (step == 0) | (strip > 0)
+
+        def joined_with(ks, rows):
             return functools.reduce(
                 jnp.add,
                 [
                     jnp.dot(
-                        front_slots[step, k],
+                        front_slots[step, k, rows],
                         couple[panel(behind(k)), :],
                         preferred_element_type=F32,
                     )
@@ -259,79 +276,92 @@
                 ],
             )
 
-        expected = (step == 0) | (strip > 0)
-
-        @pl.when(expected)
-        def _():
-            landed(front_slots.at[step, pl.ds(0, len(near))], near_sems.at[step])
-
-        joined = joined_with([0, *near])
-
-        @pl.when(expected)
-        def _():
-            landed(front_slots.at[step, pl.ds(0, len(far))], far_sems.at[step])
-
-        joined = joined + joined_with(far)
-
-        landed(load_slots.at[step, pl.ds(1, fronts - 1)], load_sems.at[step])
-        total = load_own[step]
-        for k in peers:
-            total = total + load_slots[step, k].astype(F32)
-        reduced = (total - joined).astype(BF16)
-
-        def sums_for(where):
-            return jnp.dot(reduced, inverse[:, panel(where)], preferred_element_type=F32)
-
-        for batch in batches:
-            for k in batch:
-                sum_send[step, k] = sums_for(ahead(k)).astype(BF16)
-            for k in batch:
-                send(
-                    sum_send.at[step, k],
-                    sum_slots.at[step, k],
-                    send_sems.at[3],
-                    sum_sems.at[step],
-                    (strip, ahead(k)),
-                )
-        summed = sums_for(front)
+        for h, rows in enumerate(halves):
+
+            @pl.when(expected)
+            def _():
+                landed(front_slots.at[step, pl.ds(0, len(near)), rows], near_sems.at[step, h])
+
+            @pl.when((step > 0) & (strip > 0) & (across == 1))
+            def _():
+                landed(front_slots.at[step, 0, rows], tile_sems.at[step, h])
+
+            joined = joined_with([0, *near], rows)
+
+            @pl.when(expected)
+            def _():
+                landed(front_slots.at[step, pl.ds(0, len(far)), rows], far_sems.at[step, h])
+
+            joined = joined + joined_with(far, rows)
+
+            @pl.when(step == 0)
+            def _():
+                landed(load_slots.at[0, others, rows], load_sems.at[0 if h == 0 else STEPS])
+
+            if h == 0:
+
+                @pl.when(step > 0)
+                def _():
+                    landed(load_slots.at[step, others], load_sems.at[step])
+
+            total = load_own[step, rows]
+            for k in peers:
+                total = total + load_slots[step, k, rows].astype(F32)
+            reduced = (total - joined).astype(BF16)
+
+            def sums_for(where):
+                return jnp.dot(reduced, inverse[:, panel(where)], preferred_element_type=F32)
+
+            for batch in batches:
+                for k in batch:
+                    sum_send[step, k, rows] = sums_for(ahead(k)).astype(BF16)
+                for k in batch:
+                    send(
+                        sum_send.at[step, k, rows],
+                        sum_slots.at[step, k, rows],
+                        send_sems.at[3],
+                        sum_sems.at[step, h],
+                        (strip, ahead(k)),
+                    )
+            sum_own[rows] = sums_for(front)
 
         @pl.when(step < STEPS - 1)
         def _():
-            send_loads(step + 1, peers)
-
-        landed(sum_slots.at[step, pl.ds(1, fronts - 1)], sum_sems.at[step])
-        for k in peers:
-            summed = summed + sum_slots[step, k].astype(F32)
-        out[step] = summed.astype(BF16)
+            send_loads(step + 1, pl.ds(0, group), load_sems.at[step + 1], peers)
 
         onward = (step < STEPS - 1) & (strip < strips - 1)
-
-        @pl.when(onward & (across == 0))
-        def _():
-            for k in [*far, *near, 0]:
+        for h, rows in enumerate(halves):
+            landed(sum_slots.at[step, others, rows], sum_sems.at[step, h])
+            summed = sum_own[rows]
+            for k in peers:
+                summed = summed + sum_slots[step, k, rows].astype(F32)
+            out[step, rows] = summed.astype(BF16)
+
+            @pl.when(onward & (across == 0))
+            def _():
+                for k in [*far, *near, 0]:
+                    send(
+                        out.at[step, rows],
+                        front_slots.at[step + 1, k, rows],
+                        send_sems.at[4],
+                        tile_sems.at[step + 1, h] if k == 0 else gather_sem(step + 1, k, h),
+                        (strip + 1, ahead(k)),
+                    )
+
+            @pl.when(onward & (across == 1))
+            def _():
                 send(
-                    out.at[step],
-                    front_slots.at[step + 1, k],
+                    out.at[step, rows],
+                    front_slots.at[step + 1, 0, rows],
                     send_sems.at[4],
-                    tile_sems.at[step + 1] if k == 0 else gather_sem(step + 1, k),
-                    (strip + 1, ahead(k)),
+                    tile_sems.at[step + 1, h],
+                    (strip + 1, front),
                 )
 
-        @pl.when(onward & (across == 1))
-        def _():
-            send(
-                out.at[step],
-                front_slots.at[step + 1, 0],
-                send_sems.at[4],
-                tile_sems.at[step + 1],
-                (strip + 1, front),
-            )
-
     @pl.when(strip > 0)
     def _():
         landed(upper, upper_sems.at[0])
 
-    others = pl.ds(1, fronts - 1)
     landed(front_slots.at[0, others], send_sems.at[0])
     landed(load_slots.at[:, others], send_sems.at[1])
     landed(sum_slots.at[:, others], send_sems.at[3])
@@ -371,8 +401,8 @@
             out_specs=in_vmem,
             scratch_shapes=[
                 *[pltpu.VMEM(block.shape, block.dtype) for block in blocks],
-                pltpu.VMEM((elements, 3), jnp.int32),
-                pltpu.VMEM((elements, 3), jnp.int32),
+                pltpu.VMEM((6, elements, 128), jnp.int32),
+                pltpu.VMEM((6, elements, 128), jnp.int32),
                 pltpu.VMEM((6, elements, cases), BF16),
                 pltpu.VMEM((cases, 6 * elements + inner), BF16),
                 pltpu.VMEM((cases, 6 * elements), BF16),
@@ -384,13 +414,14 @@
                 slots,
                 slots,
                 slots,
+                pltpu.VMEM((group, width), F32),
                 dma((len(blocks),)),
                 dma((2,)),
-                dma((STEPS,)),
-                dma((STEPS,)),
-                dma((STEPS,)),
-                dma((STEPS,)),
-                dma((STEPS,)),
+                dma((STEPS + 1,)),
+                dma((STEPS, 2)),
+                dma((STEPS, 2)),
+                dma((STEPS, 2)),
+                dma((STEPS, 2)),
                 dma((5,)),
             ],
             compiler_params=pltpu.CompilerParams(collective_id=0, has_side_effects=True),

time: 69.9 us -> 65 us (0.930)
  Pallas kernels: 68.3 us -> 63.4 us
    pallas_call x1, Pallas kernels: 68.3 us -> 63.4 us  [shards(): pl.pallas_call(functools.partial(kernel, strips, fronts), out_shape=jax.S...]
where the time goes in v3:
time: 65 us; the launch traced here: 64.8 us
  Pallas kernels  63.4 us (98%)
  local copies, waits for them, and re-layouts  1.47 us (2%)
    pallas_call x1, Pallas kernels, shards(): pl.pallas_call(functools.partial(kernel, strips, fronts), out_shape=jax.S...  63.4 us
    unnamed x1, local copies, waits for them, and re-layouts  1.47 us

profile of v3, /device:TPU:384, one launch (start us, length us, event | category | flops | bytes accessed | tf_op | source)
XLA Modules:
  0.0 64.8 jit_solution(1907446737028923006)
XLA Ops:
  0.0 63.4 %shard_map.91 = bf16[4,32,256]{2,1,0:T(8,128)(2,1)} custom-call(s32[3,1,64]{2,1,0:T(1,128)} %bitcast.22, s32[3,1,64]{2,1,0:T(1,128)} %bitcast.23, bf16[6,64,128]{2,1,0:T(8,128)(2,1)} %bitcast.18, bf16[6,64,128]{2,1,0:T(8,128)(2,1)} %bitcast.19, bf16[64,128]{1,0:T(8,128)(2,1)} %bitcast.20, bf16[64,4096]{1,0:T(8,128)(2,1)} %bitcast.16, ...), custom_call_target="tpu_custom_call" | custom-call | tf_op jit(solution)/shard_map/pallas_call | solution.py:397
  63.4 1.5 %copy.11 = bf16[1,4,32,256]{3,2,1,0:T(8,128)(2,1)} copy(bf16[1,4,32,256]{3,2,1,0:T(8,128)(2,1)} %bitcast.17) | data formatting | bytes 131072

commit v4 on v3

--- a/solution.py
+++ b/solution.py
@@ -48,6 +48,7 @@
     upper,
     lhs_own,
     lhs_up,
+    own_marks,
     low_marks,
     partial,
     load_send,
@@ -129,6 +130,26 @@
     for copy in fetches:
         copy.start()
 
+    def products(jobs, height):
+        def body(*sums):
+            count = 0
+            for terms, pair in zip(jobs, zip(sums[::2], sums[1::2])):
+                for lhs, rhs in terms:
+                    unit, stage = count % 2, count // 2 % 2
+                    pltpu.matmul_push_rhs(rhs(), staging_register=stage, mxu_index=unit)
+                    pltpu.matmul_acc_lhs(pair[unit], lhs(), load_staged_rhs=stage)
+                    count += 1
+            results, count = [], 0
+            for terms, pair in zip(jobs, zip(sums[::2], sums[1::2])):
+                used = sorted({(count + i) % 2 for i in range(len(terms))})
+                count += len(terms)
+                results.append(functools.reduce(jnp.add, [pltpu.matmul_pop(pair[unit]) for unit in used]))
+            return results
+
+        return pl.run_scoped(
+            body, *[pltpu.ACC(i % 2)((height, width), F32) for i in range(2 * len(jobs))]
+        )
+
     def spread(table, ids):
         nodes = table[:, 0].T
         for j in range(6):
@@ -156,7 +177,8 @@
 
     @pl.loop(0, fronts, unroll=4)
     def _(k):
-        low_marks[k] = incidence(low_ids, ahead(k))
+        low_marks[k, : 6 * low_ids.shape[1]] = incidence(low_ids, ahead(k))
+        low_marks[k, 6 * low_ids.shape[1] :] = jnp.zeros((2 * width - 6 * low_ids.shape[1], width), BF16)
 
     for copy in fetches[2:7]:
         copy.wait()
@@ -196,23 +218,48 @@
         upper[...] = jnp.zeros_like(upper)
 
     edge_rows = 6 * top_loads.shape[1]
+    inner_rows = inner_loads.shape[0]
+    lhs_own[...] = jnp.zeros_like(lhs_own)
     lhs_own[:, :edge_rows] = turned(top_loads).astype(BF16)
-    lhs_own[:, edge_rows:] = (-inner_loads[...].astype(F32).T).astype(BF16)
+    lhs_own[:, edge_rows : edge_rows + inner_rows] = (-inner_loads[...].astype(F32).T).astype(BF16)
+    own_marks[...] = jnp.zeros_like(own_marks)
 
     @pl.loop(0, fronts, unroll=2)
     def _(k):
-        where = ahead(k)
-        rhs = jnp.concatenate([incidence(own_ids, where), condense[:, panel(where)]], axis=0)
-        partial[k] = jnp.dot(lhs_own[...], rhs, preferred_element_type=F32)
+        where, slot = ahead(k), k % 2
+        own_marks[slot, :edge_rows] = incidence(own_ids, where)
+        own_marks[slot, edge_rows : edge_rows + inner_rows] = condense[:, panel(where)]
+        terms = [
+            (
+                lambda at=at: lhs_own[:, at],
+                lambda at=at: own_marks[slot, at],
+            )
+            for at in (slice(0, width), slice(width, 2 * width))
+        ]
+        partial[k] = products([terms], cases)[0]
 
     @pl.when(strip < strips - 1)
     def _():
         landed(upper, upper_sems.at[1])
 
-    lhs_up[...] = turned(upper).astype(BF16)
-
-    def loads_of(k, rows):
-        return partial[k, rows] + jnp.dot(lhs_up[rows], low_marks[k], preferred_element_type=F32)
+    lhs_up[...] = jnp.zeros_like(lhs_up)
+    lhs_up[:, :edge_rows] = turned(upper).astype(BF16)
+
+    def loads_of(ks, rows):
+        jobs = [
+            [
+                (
+                    lambda at=at: lhs_up[rows, at],
+                    lambda at=at, k=k: low_marks[k, at],
+                )
+                for at in (slice(0, width), slice(width, 2 * width))
+            ]
+            for k in ks
+        ]
+        return [
+            partial[k, rows] + result
+            for k, result in zip(ks, products(jobs, rows.stop - rows.start))
+        ]
 
     def send_loads(step, rows, sem, ks):
         for k in ks:
@@ -225,21 +272,23 @@
             )
 
     for batch in batches:
-        for k in batch:
-            load_send[0, k] = loads_of(k, slice(0, group)).astype(BF16)
+        for k, result in zip(batch, loads_of(batch, slice(0, group))):
+            load_send[0, k] = result.astype(BF16)
         send_loads(0, halves[0], load_sems.at[0], batch)
     send_loads(0, halves[1], load_sems.at[STEPS], peers)
-    load_own[0] = loads_of(0, slice(0, group))
+    load_own[0] = loads_of([0], slice(0, group))[0]
 
     @pl.loop(0, fronts, unroll=2)
     def _(k):
-        rest = loads_of(k, slice(group, cases)).astype(BF16)
+        rest = loads_of([k], slice(group, cases))[0].astype(BF16)
         for step in range(1, STEPS):
             load_send[step, k] = rest[(step - 1) * group : step * group]
 
-    rest = loads_of(0, slice(group, cases))
+    rest = loads_of([0], slice(group, cases))[0]
     for step in range(1, STEPS):
         load_own[step] = rest[(step - 1) * group : step * group]
+
+    send_loads(1, pl.ds(0, group), load_sems.at[1], peers)
 
     for copy in fetches[7:]:
         copy.wait()
@@ -264,17 +313,14 @@
         expected = (step == 0) | (strip > 0)
 
         def joined_with(ks, rows):
-            return functools.reduce(
-                jnp.add,
-                [
-                    jnp.dot(
-                        front_slots[step, k, rows],
-                        couple[panel(behind(k)), :],
-                        preferred_element_type=F32,
-                    )
-                    for k in ks
-                ],
-            )
+            terms = [
+                (
+                    lambda k=k: front_slots[step, k, rows],
+                    lambda k=k: couple[panel(behind(k)), :],
+                )
+                for k in ks
+            ]
+            return products([terms], half)[0]
 
         for h, rows in enumerate(halves):
 
@@ -309,12 +355,12 @@
                 total = total + load_slots[step, k, rows].astype(F32)
             reduced = (total - joined).astype(BF16)
 
-            def sums_for(where):
-                return jnp.dot(reduced, inverse[:, panel(where)], preferred_element_type=F32)
-
             for batch in batches:
-                for k in batch:
-                    sum_send[step, k, rows] = sums_for(ahead(k)).astype(BF16)
+                wheres = [ahead(k) for k in batch] + ([front] if batch is batches[-1] else [])
+                jobs = [[(lambda: reduced, lambda w=w: inverse[:, panel(w)])] for w in wheres]
+                results = products(jobs, half)
+                for k, result in zip(batch, results):
+                    sum_send[step, k, rows] = result.astype(BF16)
                 for k in batch:
                     send(
                         sum_send.at[step, k, rows],
@@ -323,11 +369,11 @@
                         sum_sems.at[step, h],
                         (strip, ahead(k)),
                     )
-            sum_own[rows] = sums_for(front)
-
-        @pl.when(step < STEPS - 1)
+            sum_own[rows] = results[-1]
+
+        @pl.when(step < STEPS - 2)
         def _():
-            send_loads(step + 1, pl.ds(0, group), load_sems.at[step + 1], peers)
+            send_loads(step + 2, pl.ds(0, group), load_sems.at[step + 2], peers)
 
         onward = (step < STEPS - 1) & (strip < strips - 1)
         for h, rows in enumerate(halves):
@@ -404,9 +450,10 @@
                 pltpu.VMEM((6, elements, 128), jnp.int32),
                 pltpu.VMEM((6, elements, 128), jnp.int32),
                 pltpu.VMEM((6, elements, cases), BF16),
-                pltpu.VMEM((cases, 6 * elements + inner), BF16),
-                pltpu.VMEM((cases, 6 * elements), BF16),
-                pltpu.VMEM((fronts, 6 * elements, width), BF16),
+                pltpu.VMEM((cases, 2 * width), BF16),
+                pltpu.VMEM((cases, 2 * width), BF16),
+                pltpu.VMEM((2, 2 * width, width), BF16),
+                pltpu.VMEM((fronts, 2 * width, width), BF16),
                 pltpu.VMEM((fronts, cases, width), F32),
                 slots,
                 pltpu.VMEM((STEPS, group, width), F32),

time: 65 us -> 63.7 us (0.980)
  Pallas kernels: 63.4 us -> 61.9 us
    pallas_call x1, Pallas kernels: 63.4 us -> 61.9 us  [shards(): pl.pallas_call(functools.partial(kernel, strips, fronts), out_shape=jax.S...]
where the time goes in v4:
time: 63.7 us; the launch traced here: 63.4 us
  Pallas kernels  61.9 us (97%)
  local copies, waits for them, and re-layouts  1.47 us (2%)
    pallas_call x1, Pallas kernels, shards(): pl.pallas_call(functools.partial(kernel, strips, fronts), out_shape=jax.S...  61.9 us
    unnamed x1, local copies, waits for them, and re-layouts  1.47 us

profile of v4, /device:TPU:384, one launch (start us, length us, event | category | flops | bytes accessed | tf_op | source)
XLA Modules:
  0.0 63.4 jit_solution(6001901186507340012)
XLA Ops:
  0.0 61.9 %shard_map.91 = bf16[4,32,256]{2,1,0:T(8,128)(2,1)} custom-call(s32[3,1,64]{2,1,0:T(1,128)} %bitcast.22, s32[3,1,64]{2,1,0:T(1,128)} %bitcast.23, bf16[6,64,128]{2,1,0:T(8,128)(2,1)} %bitcast.18, bf16[6,64,128]{2,1,0:T(8,128)(2,1)} %bitcast.19, bf16[64,128]{1,0:T(8,128)(2,1)} %bitcast.20, bf16[64,4096]{1,0:T(8,128)(2,1)} %bitcast.16, ...), custom_call_target="tpu_custom_call" | custom-call | tf_op jit(solution)/shard_map/pallas_call | solution.py:443
  61.9 1.5 %copy.11 = bf16[1,4,32,256]{3,2,1,0:T(8,128)(2,1)} copy(bf16[1,4,32,256]{3,2,1,0:T(8,128)(2,1)} %bitcast.17) | data formatting | bytes 131072

commit v5 on v4

--- a/solution.py
+++ b/solution.py
@@ -75,7 +75,6 @@
     far = [k for k in peers if reach(k) > 2]
     near = [k for k in peers if reach(k) <= 2]
     batches = [far, near[: len(near) // 2], near[len(near) // 2 :]]
-    across = strip % 2
 
     def ahead(k):
         return ((row + k // SIDE) % SIDE) * SIDE + (col + k % SIDE) % SIDE
@@ -297,19 +296,6 @@
 
     @pl.loop(0, STEPS)
     def _(step):
-        @pl.when((step > 0) & (strip > 0) & (across == 0))
-        def _():
-            for h, rows in enumerate(halves):
-                landed(front_slots.at[step, 0, rows], tile_sems.at[step, h])
-                for k in peers:
-                    send(
-                        front_slots.at[step, 0, rows],
-                        front_slots.at[step, k, rows],
-                        send_sems.at[2],
-                        gather_sem(step, k, h),
-                        (strip, ahead(k)),
-                    )
-
         expected = (step == 0) | (strip > 0)
 
         def joined_with(ks, rows):
@@ -328,7 +314,7 @@
             def _():
                 landed(front_slots.at[step, pl.ds(0, len(near)), rows], near_sems.at[step, h])
 
-            @pl.when((step > 0) & (strip > 0) & (across == 1))
+            @pl.when((step > 0) & (strip > 0))
             def _():
                 landed(front_slots.at[step, 0, rows], tile_sems.at[step, h])
 
@@ -383,7 +369,7 @@
                 summed = summed + sum_slots[step, k, rows].astype(F32)
             out[step, rows] = summed.astype(BF16)
 
-            @pl.when(onward & (across == 0))
+            @pl.when(onward)
             def _():
                 for k in [*far, *near, 0]:
                     send(
@@ -394,16 +380,6 @@
                         (strip + 1, ahead(k)),
                     )
 
-            @pl.when(onward & (across == 1))
-            def _():
-                send(
-                    out.at[step, rows],
-                    front_slots.at[step + 1, 0, rows],
-                    send_sems.at[4],
-                    tile_sems.at[step + 1, h],
-                    (strip + 1, front),
-                )
-
     @pl.when(strip > 0)
     def _():
         landed(upper, upper_sems.at[0])
@@ -412,17 +388,9 @@
     landed(load_slots.at[:, others], send_sems.at[1])
     landed(sum_slots.at[:, others], send_sems.at[3])
 
-    @pl.when((strip > 0) & (across == 0))
-    def _():
-        landed(front_slots.at[pl.ds(1, STEPS - 1), others], send_sems.at[2])
-
-    @pl.when((strip < strips - 1) & (across == 0))
+    @pl.when(strip < strips - 1)
     def _():
         landed(front_slots.at[pl.ds(1, STEPS - 1)], send_sems.at[4])
-
-    @pl.when((strip < strips - 1) & (across == 1))
-    def _():
-        landed(front_slots.at[pl.ds(1, STEPS - 1), 0], send_sems.at[4])
 
 
 def solution(mesh):

time: 63.7 us -> 59.7 us (0.937)
  the two profiles are of different devices: /device:TPU:384 before, /device:TPU:321 now
where the time goes in v5:
time: 59.7 us; the launch traced here: 59.5 us
  Pallas kernels  58 us (97%)
  local copies, waits for them, and re-layouts  1.47 us (2%)
    pallas_call x1, Pallas kernels, shards(): pl.pallas_call(functools.partial(kernel, strips, fronts), out_shape=jax.S...  58 us
    unnamed x1, local copies, waits for them, and re-layouts  1.47 us

profile of v5, /device:TPU:321, one launch (start us, length us, event | category | flops | bytes accessed | tf_op | source)
XLA Modules:
  0.0 59.5 jit_solution(17534847131205735587)
XLA Ops:
  0.0 58.0 %shard_map.91 = bf16[4,32,256]{2,1,0:T(8,128)(2,1)} custom-call(s32[3,1,64]{2,1,0:T(1,128)} %bitcast.22, s32[3,1,64]{2,1,0:T(1,128)} %bitcast.23, bf16[6,64,128]{2,1,0:T(8,128)(2,1)} %bitcast.18, bf16[6,64,128]{2,1,0:T(8,128)(2,1)} %bitcast.19, bf16[64,128]{1,0:T(8,128)(2,1)} %bitcast.20, bf16[64,4096]{1,0:T(8,128)(2,1)} %bitcast.16, ...), custom_call_target="tpu_custom_call" | custom-call | tf_op jit(solution)/shard_map/pallas_call | solution.py:411
  58.0 1.5 %copy.11 = bf16[1,4,32,256]{3,2,1,0:T(8,128)(2,1)} copy(bf16[1,4,32,256]{3,2,1,0:T(8,128)(2,1)} %bitcast.17) | data formatting | bytes 131072
